TPU v7x, 32 devices: a whole 2x2x4 slice. The times are simulated.
32 devices in a mesh: ep: 4 (over y, x), tp: 8 (over z, core).
Axes of the slice: x: 2, y: 2, z: 4, core: 2. Of those that a mesh axis runs over, the one named last changes fastest.
Arguments:
- tokens: bfloat16 [512, 6144], P('ep'), may hold values from -6 to 6
- expert_ids: int32 [512, 2], P('ep'), may hold values from 0 to 3, all different within a row; in each aligned block of 128 rows (0 to 127, 128 to 255, ...) at most 96 rows name the same one
- router: bfloat16 [6144, 4], replicated, may hold values from -0.078125 to 0.078125
- gate_weight: bfloat16 [4, 6144, 8192], P('ep', None, 'tp'), may hold values from -0.078125 to 0.078125
- up_weight: bfloat16 [4, 6144, 8192], P('ep', None, 'tp'), may hold values from -0.078125 to 0.078125
- down_weight: bfloat16 [4, 8192, 6144], P('ep', 'tp'), may hold values from -0.0625 to 0.0625
- keep_mask: int32 [512, 6144], P('ep'), may hold values 0 or 1
Outputs:
- layer_out: bfloat16 [512, 6144], P('ep')
Inputs may be any that keep to these rules, and one draw needn't show every extreme that they name: `expert_ids`: each row names two different experts. In the rows of one token block of 128 rows no expert is named more than 96 times, a bound that some block reaches.
All inputs are finite; a program needn't handle non-finite values. No bound on the sum of `keep_mask` on one device may be relied on, other than what follows from the above.
Results may differ from a plain program's by a relative error of at most 0.018.
Values may be sent and summed in bfloat16 or wider, within the bound.
A program may use at most 128 MiB of HBM per device.

v0:
```python
import jax
import jax.numpy as jnp
from jax import lax
from jax.sharding import PartitionSpec as P


def shards(tokens, expert_ids, router, gate_weight, up_weight, down_weight, keep_mask):
    experts = router.shape[1]
    tok_rows = tokens.shape[0]
    width_model = tokens.shape[1]
    capacity = 3 * tok_rows // experts
    groups = lax.axis_size("tp")
    share = capacity // groups
    logits = jnp.dot(tokens, router, preferred_element_type=jnp.float32)
    picked = jnp.take_along_axis(logits, expert_ids, axis=1)
    weight_first = jax.nn.sigmoid(picked[:, 0] - picked[:, 1])
    weight_second = jax.nn.sigmoid(picked[:, 1] - picked[:, 0])
    onehot = (expert_ids[:, :, None] == jnp.arange(experts, dtype=jnp.int32)[None, None, :]).astype(
        jnp.int32
    )
    onehot = onehot.reshape(tok_rows * 2, experts)
    ranks = jnp.cumsum(onehot, axis=0) - onehot
    slot = jnp.sum(ranks * onehot, axis=1).reshape(tok_rows, 2)
    place = slot * experts + expert_ids
    lines = jnp.arange(experts * capacity, dtype=jnp.int32)
    picker = ((place[None, :, 0] == lines[:, None]) | (place[None, :, 1] == lines[:, None])).astype(
        jnp.bfloat16
    )
    outgoing = jnp.dot(picker, tokens, preferred_element_type=jnp.float32).astype(jnp.bfloat16)
    outgoing = outgoing.reshape(capacity, experts, width_model)
    w_gate = gate_weight[0]
    w_up = up_weight[0]
    w_down = down_weight[0]
    arrived = lax.all_to_all(outgoing, "ep", split_axis=1, concat_axis=1, tiled=True)
    rows = arrived.reshape(capacity * experts, width_model)
    gate = jnp.dot(rows, w_gate, preferred_element_type=jnp.float32)
    up = jnp.dot(rows, w_up, preferred_element_type=jnp.float32)
    hidden = (jax.nn.silu(gate) * up).astype(jnp.bfloat16)
    summed = lax.psum_scatter(
        jnp.dot(hidden, w_down, preferred_element_type=jnp.float32).astype(jnp.bfloat16),
        "tp",
        scatter_dimension=0,
        tiled=True,
    )
    expert_out = summed.reshape(share, experts, width_model)
    back = lax.all_to_all(expert_out, "ep", split_axis=1, concat_axis=1, tiled=True)
    returned = lax.all_gather(back, "tp", axis=0, tiled=True)
    returned = returned.reshape(capacity * experts, width_model)
    first_rows = jnp.take(returned, place[:, 0], axis=0).astype(jnp.float32)
    second_rows = jnp.take(returned, place[:, 1], axis=0).astype(jnp.float32)
    combined = weight_first[:, None] * first_rows + weight_second[:, None] * second_rows
    return (combined * keep_mask.astype(jnp.float32) * 1.25).astype(jnp.bfloat16)


def solution(mesh):
    return jax.shard_map(
        shards,
        mesh=mesh,
        in_specs=(
            P("ep", None),
            P("ep", None),
            P(),
            P("ep", None, "tp"),
            P("ep", None, "tp"),
            P("ep", "tp", None),
            P("ep", None),
        ),
        out_specs=P("ep", None),
        check_vma=False,
    )
```

profile of v0, /device:TPU:0, one launch (start us, length us, event | category | flops | bytes accessed | tf_op | source)
XLA Modules:
  0.0 282.0 jit_solution(14242153663635588185)
XLA Ops:
  6.5 0.0 copy-start
  6.5 0.0 reduce-scatter.2.cloned.1.call-start
  6.5 0.9 copy.59
  7.4 0.1 eq.60
  7.6 0.1 eq.56
  7.7 1.2 reduce-window.6
  9.0 0.1 slice.34
  9.0 0.1 copy.61
  9.2 0.1 copy.62
  9.3 0.1 add_bitcast_fusion
  9.4 0.1 mul.50
  9.6 0.2 slice_reduce_fusion.1
  9.7 0.0 copy-start.2
  9.7 0.0 copy-start.4
  9.8 0.6 copy-done.2
  10.3 0.0 copy-done.4
  10.3 0.0 copy-done
  10.3 3.5 %convolution_convert_fusion = bf16[384,6144]{1,0:T(8,128)(2,1)} fusion(bf16[128,6144]{1,0:T(8,128)(2,1)S(1)} %copy-done, s32[128]{0:T(128)S(1)} %get-tuple-element.7, s32[128]{0:T(128)S(1)} %get-tuple-element.6), kind=kOutput, calls=%fused_computation.10 | convolution fusion | flops 606486528 | bytes 6292480 | tf_op jit(solution)/shard_map/dot_general | solution.py:29
  13.8 7.6 %reshape.51 = bf16[96,4,6144]{2,1,0:T(4,128)(2,1)} reshape(bf16[384,6144]{1,0:T(8,128)(2,1)} %convolution_convert_fusion) | data formatting | bytes 9437184 | tf_op jit(solution)/shard_map/reshape | solution.py:30
  21.4 4.9 %copy.64 = bf16[96,4,6144]{2,0,1:T(8,128)(2,1)S(1)} copy(bf16[96,4,6144]{2,1,0:T(4,128)(2,1)} %reshape.51) | data formatting | bytes 9437184 | tf_op jit(solution)/shard_map/reshape | solution.py:30
  26.3 58.5 %all_to_all.10 = bf16[96,4,6144]{2,0,1:T(8,128)(2,1)S(1)} all-to-all(bf16[96,4,6144]{2,0,1:T(8,128)(2,1)S(1)} %copy.64), channel_id=1, replica_groups=mesh['ep'=4,'tp'=8] {'ep'}, dimensions={1} | all-to-all | bytes 9437184 | tf_op jit(solution)/shard_map/all_to_all | solution.py:34
  84.8 5.8 %copy.65 = bf16[96,4,6144]{2,1,0:T(4,128)(2,1)} copy(bf16[96,4,6144]{2,0,1:T(8,128)(2,1)S(1)} %all_to_all.10) | data formatting | bytes 9437184 | tf_op jit(solution)/shard_map/all_to_all | solution.py:34
  90.6 7.2 %reshape.52 = bf16[384,6144]{1,0:T(8,128)(2,1)} reshape(bf16[96,4,6144]{2,1,0:T(4,128)(2,1)} %copy.65) | data formatting | bytes 9437184 | tf_op jit(solution)/shard_map/reshape | solution.py:35
  97.8 9.6 %fusion.4 = f32[384,1024]{1,0:T(8,128)S(1)} fusion(bf16[384,6144]{1,0:T(8,128)(2,1)} %reshape.52, bf16[1,6144,1024]{2,1,0:T(8,128)(2,1)} %param.12), kind=kOutput, calls=%fused_computation.7 | convolution fusion | flops 4831838208 | bytes 18874368 | tf_op jit(solution)/shard_map/dot_general | solution.py:36
  107.3 21.7 %fusion.6 = bf16[384,6144]{1,0:T(8,128)(2,1)} fusion(bf16[1,1024,6144]{2,1,0:T(8,128)(2,1)} %param.14, f32[384,1024]{1,0:T(8,128)S(1)} %fusion.4, bf16[384,6144]{1,0:T(8,128)(2,1)} %reshape.52, bf16[1,6144,1024]{2,1,0:T(8,128)(2,1)} %param.13), kind=kOutput, calls=%fused_computation.9 | convolution fusion | flops 9668395008 | bytes 36175872 | tf_op jit(solution)/shard_map/dot_general | solution.py:40
  129.0 0.0 reduce-scatter.2.cloned.1.call-update
  129.0 0.0 copy-start.6
  129.1 0.0 copy-start.1
  129.1 0.0 all-gather.2.cloned.1.call-start
  129.1 54.7 %reduce-scatter.2.cloned.1.call-done = bf16[48,6144]{1,0:T(8,128)(2,1)} async-done(((bf16[384,6144]{1,0:T(8,128)(2,1)}), bf16[48,6144]{1,0:T(8,128)(2,1)}) %reduce-scatter.2.cloned.1.call-update) | async-done | bytes 589840 | tf_op jit(solution)/shard_map/reduce_scatter | solution.py:39
  183.8 1.3 reshape.53
  185.1 0.3 copy.66
  185.4 12.9 %all_to_all.11 = bf16[12,4,6144]{2,0,1:T(8,128)(2,1)S(1)} all-to-all(bf16[12,4,6144]{2,0,1:T(8,128)(2,1)S(1)} %copy.66), channel_id=1, replica_groups=mesh['ep'=4,'tp'=8] {'ep'}, dimensions={1} | all-to-all | bytes 1179648 | tf_op jit(solution)/shard_map/all_to_all | solution.py:46
  198.3 1.3 copy.67
  199.6 0.0 all-gather.2.cloned.1.call-update
  199.6 0.0 copy-done.6
  199.6 0.1 copy.57
  199.7 0.1 reshape.71
  199.9 0.0 copy-done.1
  199.9 0.5 fusion.22
  200.4 0.0 copy-start.3
  200.4 0.0 copy-start.5
  200.4 2.4 gather_fusion
  202.8 0.1 reshape.74
  202.9 0.1 copy.58
  203.0 0.0 copy-done.3
  203.0 0.0 copy-done.5
  203.1 46.7 %all-gather.2.cloned.1.call-done = bf16[96,4,6144]{2,1,0:T(4,128)(2,1)} async-done(((bf16[12,4,6144]{2,1,0:T(4,128)(2,1)}), bf16[96,4,6144]{2,1,0:T(4,128)(2,1)}) %all-gather.2.cloned.1.call-update) | async-done | bytes 4718608 | tf_op jit(solution)/shard_map/all_gather | solution.py:47
  249.9 7.2 %reshape.54 = bf16[384,6144]{1,0:T(8,128)(2,1)} reshape(bf16[96,4,6144]{2,1,0:T(4,128)(2,1)} %all-gather.2.cloned.1.call-done) | data formatting | bytes 9437184 | tf_op jit(solution)/shard_map/reshape | solution.py:48
  257.1 5.9 %gather_fusion.1 = bf16[128,6144]{1,0:T(8,128)(2,1)S(1)} fusion(bf16[384,6144]{1,0:T(8,128)(2,1)} %reshape.54, s32[1024]{0:T(1024)S(1)} %pad_clamp_fusion.1), kind=kCustom, calls=%fused_computation.clone | custom fusion | bytes 3146240 | tf_op jit(solution)/shard_map/jit(_take)/gather | solution.py:49
  263.1 7.1 %gather_fusion.2 = bf16[128,6144]{1,0:T(8,128)(2,1)} fusion(bf16[384,6144]{1,0:T(8,128)(2,1)} %reshape.54, s32[1024]{0:T(1024)S(1)} %pad_clamp_fusion), kind=kCustom, calls=%fused_computation.1.clone | custom fusion | bytes 3146240 | tf_op jit(solution)/shard_map/jit(_take)/gather | solution.py:50
  270.2 5.0 %multiply_convert_fusion = bf16[128,6144]{1,0:T(8,128)(2,1)} fusion(s32[128,6144]{1,0:T(8,128)} %param.15, bf16[128,6144]{1,0:T(8,128)(2,1)} %gather_fusion.2, bf16[128,6144]{1,0:T(8,128)(2,1)S(1)} %gather_fusion.1, f32[128]{0:T(128)S(1)} %get-tuple-element.9, f32[128]{0:T(128)S(1)} %get-tuple-element.8, pred[128]{0:T(512)(128)(4,1)S(1)} %get-tuple-element.12, ...), kind=kLoop, calls=%fused_computation.11 | loop fusion | flops 8650752 | bytes 7865600 | tf_op jit(solution)/shard_map/convert_element_type | solution.py:52
  (13 shorter events, 0.1 us)
Async XLA Ops:
  6.5 3.8 %copy-start = (bf16[128,6144]{1,0:T(8,128)(2,1)S(1)}, bf16[128,6144]{1,0:T(8,128)(2,1)}, u32[]{:S(2)}) copy-start(bf16[128,6144]{1,0:T(8,128)(2,1)} %param.9) | copy-start | bytes 4718596
  6.5 177.2 %reduce-scatter.2.cloned.1.call-start = ((), (), s32[]{:S(2)}) async-start(), calls=%async_computation.3 | async-start | bytes 5308416 | tf_op jit(solution)/shard_map/reduce_scatter | solution.py:39
  9.7 0.6 copy-start.2
  9.7 0.6 copy-start.4
  129.0 70.6 %copy-start.6 = (s32[128,2]{0,1:T(2,128)S(1)}, s32[128,2]{0,1:T(2,128)}, u32[]{:S(2)}) copy-start(s32[128,2]{0,1:T(2,128)} %param.10) | copy-start | bytes 3076
  129.1 70.8 %copy-start.1 = (bf16[6144,4]{0,1:T(4,128)(2,1)S(1)}, bf16[6144,4]{0,1:T(4,128)(2,1)}, u32[]{:S(2)}) copy-start(bf16[6144,4]{0,1:T(4,128)(2,1)} %param.11) | copy-start | bytes 147460
  129.1 120.8 %all-gather.2.cloned.1.call-start = ((), (), s32[]{:S(2)}) async-start(), calls=%async_computation.4 | async-start | bytes 5308416 | tf_op jit(solution)/shard_map/all_gather | solution.py:47
  200.4 2.6 copy-start.3
  200.4 2.6 copy-start.5
Sparse Core Ops, SparseCore 0:
  129.2 54.5 reduce-scatter.1
  199.7 50.0 all-gather.1
where the time goes:
time: 283 us; the launch traced here: 282 us
  waiting for transfers between devices  101 us (36%)
  blocking collectives  71.4 us (25%)
  local copies, waits for them, and re-layouts  53.9 us (19%)
  matrix products  35.2 us (12%)
  between operations  13.6 us (5%)
  other arithmetic  6.43 us (2%)
    all_to_all x1, blocking collectives, shards(): lax.all_to_all(outgoing, 'ep', split_axis=1, concat_axis=1, tiled=True)  58.5 us
    reduce_scatter x1, waiting for transfers between devices, shards(): lax.psum_scatter(jnp.dot(hidden, w_down, preferred_element_type=jnp.float...  54.7 us
    all_gather x1, waiting for transfers between devices, shards(): returned = lax.all_gather(back, 'tp', axis=0, tiled=True)  46.7 us
    dot_general x1, matrix products, shards(): jnp.dot(hidden, w_down, preferred_element_type=jnp.float32)  21.7 us
    all_to_all x1, blocking collectives, shards(): lax.all_to_all(expert_out, 'ep', split_axis=1, concat_axis=1, tiled=True)  12.9 us
    reshape x2, local copies, waits for them, and re-layouts, shards(): outgoing = outgoing.reshape(capacity, experts, width_model)  12.5 us
    dot_general x1, matrix products, shards(): gate = jnp.dot(rows, w_gate, preferred_element_type=jnp.float32)  9.55 us
    reshape x1, local copies, waits for them, and re-layouts, shards(): returned = returned.reshape(capacity * experts, width_model)  7.25 us
  transfers between devices with their start and end apart: 2, of which 2 were waited for; matrix products, arithmetic and copies ran while one was open for 1% of the time, Pallas kernels for 0%

commit v1 on v0

--- a/solution.py
+++ b/solution.py
@@ -1,7 +1,24 @@
+import functools
 import jax
 import jax.numpy as jnp
 from jax import lax
 from jax.sharding import PartitionSpec as P
+
+
+def move_stops_all_over_axis(local_array, mesh_ax):
+    wide_out = jnp.concatenate(
+        jax.lax.all_to_all(
+            jnp.stack(jnp.split(local_array, jax.lax.axis_size(mesh_ax), axis=1)),
+            mesh_ax,
+            split_axis=0,
+            concat_axis=0,
+        ),
+        axis=1,
+    )
+    return wide_out
+
+
+view_compute = functools.partial(move_stops_all_over_axis, mesh_ax="ep")
 
 
 def shards(tokens, expert_ids, router, gate_weight, up_weight, down_weight, keep_mask):
@@ -31,7 +48,7 @@
     w_gate = gate_weight[0]
     w_up = up_weight[0]
     w_down = down_weight[0]
-    arrived = lax.all_to_all(outgoing, "ep", split_axis=1, concat_axis=1, tiled=True)
+    arrived = view_compute(outgoing)
     rows = arrived.reshape(capacity * experts, width_model)
     gate = jnp.dot(rows, w_gate, preferred_element_type=jnp.float32)
     up = jnp.dot(rows, w_up, preferred_element_type=jnp.float32)

time: 283 us -> 297 us (1.049)
  local copies, waits for them, and re-layouts: 53.9 us -> 67.2 us
    split x0 -> x1, local copies, waits for them, and re-layouts: none -> 15.5 us  [move_stops_all_over_axis(): jnp.split(local_array, jax.lax.axis_size(mesh_ax), axis=1)]
    another operation x2 -> x5, local copies, waits for them, and re-layouts: 0.1 us -> 9.97 us  [the longest x1 7.22 us: shards(): rows = arrived.reshape(capacity * experts, width_model)]
    all_to_all x1 -> x0, local copies, waits for them, and re-layouts: 5.81 us -> none  [shards(): lax.all_to_all(outgoing, 'ep', split_axis=1, concat_axis=1, tiled=True)]
    reshape x2 -> x1, local copies, waits for them, and re-layouts: 12.5 us -> 7.59 us  [shards(): outgoing = outgoing.reshape(capacity, experts, width_model)]
where the time goes in v1:
time: 297 us; the launch traced here: 296 us
  waiting for transfers between devices  102 us (34%)
  blocking collectives  71.3 us (24%)
  local copies, waits for them, and re-layouts  67.2 us (23%)
  matrix products  35.3 us (12%)
  between operations  13.6 us (5%)
  other arithmetic  7.07 us (2%)
    all_to_all x1, blocking collectives, move_stops_all_over_axis(): jax.lax.all_to_all(jnp.stack(jnp.split(local_array, jax.lax.axis_size(mes...  58.5 us
    reduce_scatter x1, waiting for transfers between devices, shards(): lax.psum_scatter(jnp.dot(hidden, w_down, preferred_element_type=jnp.float...  54.7 us
    all_gather x1, waiting for transfers between devices, shards(): returned = lax.all_gather(back, 'tp', axis=0, tiled=True)  46.8 us
    dot_general x1, matrix products, shards(): jnp.dot(hidden, w_down, preferred_element_type=jnp.float32)  21.7 us
    split x1, local copies, waits for them, and re-layouts, move_stops_all_over_axis(): jnp.split(local_array, jax.lax.axis_size(mesh_ax), axis=1)  15.5 us
    all_to_all x1, blocking collectives, shards(): lax.all_to_all(expert_out, 'ep', split_axis=1, concat_axis=1, tiled=True)  12.9 us
    dot_general x1, matrix products, shards(): gate = jnp.dot(rows, w_gate, preferred_element_type=jnp.float32)  9.59 us
    reshape x1, local copies, waits for them, and re-layouts, shards(): outgoing = outgoing.reshape(capacity, experts, width_model)  7.59 us
  transfers between devices with their start and end apart: 2, of which 2 were waited for; matrix products, arithmetic and copies ran while one was open for 1% of the time, Pallas kernels for 0%

profile of v1, /device:TPU:0, one launch (start us, length us, event | category | flops | bytes accessed | tf_op | source)
XLA Modules:
  0.0 296.0 jit_solution(806544178255644599)
XLA Ops:
  6.5 0.0 copy-start
  6.5 0.0 reduce-scatter.2.cloned.1.call-start
  6.5 0.9 copy.62
  7.4 0.1 eq.60
  7.6 0.1 eq.56
  7.7 1.2 reduce-window.6
  9.0 0.1 slice.34
  9.0 0.1 copy.64
  9.2 0.1 copy.65
  9.3 0.1 add_bitcast_fusion
  9.4 0.1 mul.50
  9.6 0.2 slice_reduce_fusion.1
  9.7 0.0 copy-start.2
  9.7 0.0 copy-start.4
  9.8 0.6 copy-done.2
  10.3 0.0 copy-done.4
  10.3 0.0 copy-done
  10.3 3.5 %convolution_convert_fusion = bf16[384,6144]{1,0:T(8,128)(2,1)} fusion(bf16[128,6144]{1,0:T(8,128)(2,1)S(1)} %copy-done, s32[128]{0:T(128)S(1)} %get-tuple-element.7, s32[128]{0:T(128)S(1)} %get-tuple-element.6), kind=kOutput, calls=%fused_computation.10 | convolution fusion | flops 606486528 | bytes 6292480 | tf_op jit(solution)/shard_map/dot_general | solution.py:46
  13.8 7.6 %reshape.51 = bf16[96,4,6144]{2,1,0:T(4,128)(2,1)} reshape(bf16[384,6144]{1,0:T(8,128)(2,1)} %convolution_convert_fusion) | data formatting | bytes 9437184 | tf_op jit(solution)/shard_map/reshape | solution.py:47
  21.4 15.5 %fusion.22 = (bf16[96,1,6144]{2,1,0:T(2,128)(2,1)S(1)}, bf16[96,1,6144]{2,1,0:T(2,128)(2,1)S(1)}, bf16[96,1,6144]{2,1,0:T(2,128)(2,1)S(1)}, bf16[96,1,6144]{2,1,0:T(2,128)(2,1)S(1)}) fusion(bf16[96,4,6144]{2,1,0:T(4,128)(2,1)} %reshape.51), kind=kLoop, calls=%fused_computation.46 | loop fusion | bytes 9437184 | tf_op jit(solution)/shard_map/split | solution.py:11
  36.9 1.3 copy_bitcast_fusion.2
  38.2 1.3 copy_bitcast_fusion
  39.6 0.6 pad_maximum_fusion
  40.2 58.5 %all_to_all.10 = bf16[4,96,1,6144]{3,1,2,0:T(8,128)(2,1)S(1)} all-to-all(bf16[4,96,1,6144]{3,1,2,0:T(8,128)(2,1)S(1)} %pad_maximum_fusion), channel_id=1, replica_groups=mesh['ep'=4,'tp'=8] {'ep'}, dimensions={0} | all-to-all | bytes 9437184 | tf_op jit(solution)/shard_map/all_to_all | solution.py:10
  98.7 5.8 %copy.71 = bf16[96,4,1,6144]{3,1,0,2:T(4,128)(2,1)} copy(bf16[96,4,1,6144]{3,0,2,1:T(8,128)(2,1)S(1)} %bitcast.58) | data formatting | bytes 9437184 | tf_op jit(solution)/shard_map/reshape | solution.py:9
  104.5 7.2 %reshape_reshape.3 = bf16[384,6144]{1,0:T(8,128)(2,1)} reshape(bf16[96,4,1,6144]{3,1,0,2:T(4,128)(2,1)} %copy.71) | data formatting | bytes 9437184 | tf_op jit(solution)/shard_map/reshape;reshape | solution.py:52
  111.7 9.6 %fusion.4 = f32[384,1024]{1,0:T(8,128)S(1)} fusion(bf16[384,6144]{1,0:T(8,128)(2,1)} %reshape_reshape.3, bf16[1,6144,1024]{2,1,0:T(8,128)(2,1)} %param.12), kind=kOutput, calls=%fused_computation.7 | convolution fusion | flops 4831838208 | bytes 18874368 | tf_op jit(solution)/shard_map/dot_general | solution.py:53
  121.3 21.7 %fusion.6 = bf16[384,6144]{1,0:T(8,128)(2,1)} fusion(bf16[1,1024,6144]{2,1,0:T(8,128)(2,1)} %param.14, f32[384,1024]{1,0:T(8,128)S(1)} %fusion.4, bf16[384,6144]{1,0:T(8,128)(2,1)} %reshape_reshape.3, bf16[1,6144,1024]{2,1,0:T(8,128)(2,1)} %param.13), kind=kOutput, calls=%fused_computation.9 | convolution fusion | flops 9668395008 | bytes 36175872 | tf_op jit(solution)/shard_map/dot_general | solution.py:57
  143.0 0.0 reduce-scatter.2.cloned.1.call-update
  143.0 0.0 all-gather.2.cloned.1.call-start
  143.0 54.7 %reduce-scatter.2.cloned.1.call-done = bf16[48,6144]{1,0:T(8,128)(2,1)} async-done(((bf16[384,6144]{1,0:T(8,128)(2,1)}), bf16[48,6144]{1,0:T(8,128)(2,1)}) %reduce-scatter.2.cloned.1.call-update) | async-done | bytes 589840 | tf_op jit(solution)/shard_map/reduce_scatter | solution.py:56
  197.8 1.3 reshape.53
  199.0 0.0 copy-start.6
  199.1 0.0 copy-start.1
  199.1 0.3 copy.72
  199.4 12.9 %all_to_all.11 = bf16[12,4,6144]{2,0,1:T(8,128)(2,1)S(1)} all-to-all(bf16[12,4,6144]{2,0,1:T(8,128)(2,1)S(1)} %copy.72), channel_id=1, replica_groups=mesh['ep'=4,'tp'=8] {'ep'}, dimensions={1} | all-to-all | bytes 1179648 | tf_op jit(solution)/shard_map/all_to_all | solution.py:63
  212.3 1.3 copy.73
  213.6 0.0 all-gather.2.cloned.1.call-update
  213.6 0.0 copy-done.6
  213.6 0.1 copy.60
  213.7 0.1 reshape.71
  213.9 0.0 copy-done.1
  213.9 0.5 fusion.23
  214.4 0.0 copy-start.3
  214.4 0.0 copy-start.5
  214.4 2.4 gather_fusion
  216.8 0.1 reshape.74
  216.9 0.1 copy.61
  217.0 0.0 copy-done.3
  217.0 0.0 copy-done.5
  217.1 46.8 %all-gather.2.cloned.1.call-done = bf16[96,4,6144]{2,1,0:T(4,128)(2,1)} async-done(((bf16[12,4,6144]{2,1,0:T(4,128)(2,1)}), bf16[96,4,6144]{2,1,0:T(4,128)(2,1)}) %all-gather.2.cloned.1.call-update) | async-done | bytes 4718608 | tf_op jit(solution)/shard_map/all_gather | solution.py:64
  263.9 7.3 %reshape.54 = bf16[384,6144]{1,0:T(8,128)(2,1)} reshape(bf16[96,4,6144]{2,1,0:T(4,128)(2,1)} %all-gather.2.cloned.1.call-done) | data formatting | bytes 9437184 | tf_op jit(solution)/shard_map/reshape | solution.py:65
  271.1 5.9 %gather_fusion.1 = bf16[128,6144]{1,0:T(8,128)(2,1)S(1)} fusion(bf16[384,6144]{1,0:T(8,128)(2,1)} %reshape.54, s32[1024]{0:T(1024)S(1)} %pad_clamp_fusion.1), kind=kCustom, calls=%fused_computation.clone | custom fusion | bytes 3146240 | tf_op jit(solution)/shard_map/jit(_take)/gather | solution.py:66
  277.1 7.1 %gather_fusion.2 = bf16[128,6144]{1,0:T(8,128)(2,1)} fusion(bf16[384,6144]{1,0:T(8,128)(2,1)} %reshape.54, s32[1024]{0:T(1024)S(1)} %pad_clamp_fusion), kind=kCustom, calls=%fused_computation.1.clone | custom fusion | bytes 3146240 | tf_op jit(solution)/shard_map/jit(_take)/gather | solution.py:67
  284.1 5.0 %multiply_convert_fusion = bf16[128,6144]{1,0:T(8,128)(2,1)} fusion(s32[128,6144]{1,0:T(8,128)} %param.15, bf16[128,6144]{1,0:T(8,128)(2,1)} %gather_fusion.2, bf16[128,6144]{1,0:T(8,128)(2,1)S(1)} %gather_fusion.1, f32[128]{0:T(128)S(1)} %get-tuple-element.13, f32[128]{0:T(128)S(1)} %get-tuple-element.12, pred[128]{0:T(512)(128)(4,1)S(1)} %get-tuple-element.16, ...), kind=kLoop, calls=%fused_computation.12 | loop fusion | flops 8650752 | bytes 7865600 | tf_op jit(solution)/shard_map/convert_element_type | solution.py:69
  (13 shorter events, 0.1 us)
Async XLA Ops:
  6.5 3.8 %copy-start = (bf16[128,6144]{1,0:T(8,128)(2,1)S(1)}, bf16[128,6144]{1,0:T(8,128)(2,1)}, u32[]{:S(2)}) copy-start(bf16[128,6144]{1,0:T(8,128)(2,1)} %param.9) | copy-start | bytes 4718596
  6.5 191.2 %reduce-scatter.2.cloned.1.call-start = ((), (), s32[]{:S(2)}) async-start(), calls=%async_computation.3 | async-start | bytes 5308416 | tf_op jit(solution)/shard_map/reduce_scatter | solution.py:56
  9.7 0.6 copy-start.2
  9.7 0.6 copy-start.4
  143.0 120.9 %all-gather.2.cloned.1.call-start = ((), (), s32[]{:S(2)}) async-start(), calls=%async_computation.4 | async-start | bytes 5308416 | tf_op jit(solution)/shard_map/all_gather | solution.py:64
  199.0 14.5 %copy-start.6 = (s32[128,2]{0,1:T(2,128)S(1)}, s32[128,2]{0,1:T(2,128)}, u32[]{:S(2)}) copy-start(s32[128,2]{0,1:T(2,128)} %param.10) | copy-start | bytes 3076
  199.1 14.8 %copy-start.1 = (bf16[6144,4]{0,1:T(4,128)(2,1)S(1)}, bf16[6144,4]{0,1:T(4,128)(2,1)}, u32[]{:S(2)}) copy-start(bf16[6144,4]{0,1:T(4,128)(2,1)} %param.11) | copy-start | bytes 147460
  214.4 2.6 copy-start.3
  214.4 2.6 copy-start.5
Sparse Core Ops, SparseCore 0:
  143.1 54.5 reduce-scatter.1
  213.7 50.0 all-gather.1
